TPU v7x, 256 devices: a whole 4x4x8 slice. The times are simulated.
256 devices in a mesh: src: 16 (over x_hi, z), tgt: 16 (over x_lo, y, core).
Axes of the slice: x: 4 (x_hi: 2, x_lo: 2; x = x_hi * 2 + x_lo), y: 4, z: 8, core: 2. Of those that a mesh axis runs over, the one named last changes fastest.
Arguments:
- source_words: bfloat16 [32768, 300], P(('src', 'tgt')), may hold values from -3 to 3
- target_words: bfloat16 [30720, 300], P(('tgt', 'src')), may hold values from -24 to 24
Outputs:
- rotated: bfloat16 [32768, 300], P(('src', 'tgt'))
- matched: float32 [32768, 300], P(('src', 'tgt'))
- ortho: float32 [300, 300], replicated
- row_pot: float32 [32768], P(('src', 'tgt'))
- col_pot: float32 [30720], P(('tgt', 'src'))
All inputs are finite; a program needn't handle non-finite values.
Results may differ from a plain program's by a relative error of at most 0.0034.
Values may be sent and summed in bfloat16 or wider, within the bound.
A program may use at most 64 MiB of HBM per device.

v0:
```python
import math
import jax
import jax.numpy as jnp
from jax import lax
from jax.sharding import PartitionSpec as P

ITERS = 2
NEWTON = 12


def sent_to_all(array, axis):
    copies = jnp.broadcast_to(array, (lax.axis_size(axis), *array.shape))
    return lax.all_to_all(copies, axis, split_axis=0, concat_axis=0, tiled=True)


def collected_together(array, axis):
    leaves = jax.tree.leaves(array)
    sequence = sorted(range(len(leaves)), key=lambda k: -leaves[k].size)
    width = (1, *leaves[sequence[0]].shape)[-1]
    lines = [
        jnp.pad(leaves[k].reshape(-1), (0, -leaves[k].size % width)).reshape(-1, width)
        for k in sequence
    ]
    both, at, found = (sent_to_all(jnp.concatenate(lines), axis), 0, {})
    for k, line in zip(sequence, lines):
        share = both[:, at : at + len(line)].reshape(len(both), -1)
        found[k] = share[:, : leaves[k].size].reshape(-1, *leaves[k].shape)
        at += len(line)
    numbers = iter(range(len(leaves)))
    return jax.tree.map(lambda _: found[next(numbers)], array)


def folded_in_pairs(pieces, combine):
    while len(jax.tree.leaves(pieces)[0]) > 1:
        pieces = jax.vmap(combine)(
            *(jax.tree.map(lambda part: part[side::2], pieces) for side in (0, 1))
        )
    return jax.tree.map(lambda part: part[0], pieces)


def combined_all(array, axis, combine):
    pieces = collected_together(array, axis)
    return folded_in_pairs(pieces, combine)


def gathered_by_type(array, axis):
    leaves, found = (jax.tree.leaves(array), {})
    for first, a in enumerate(leaves):
        if first not in found:
            alike = [k for k, b in enumerate(leaves) if b.dtype == a.dtype]
            got = (
                collected_together([leaves[k] for k in alike], axis)
                if len(alike) > 1
                else [sent_to_all(a, axis)]
            )
            for k, b in zip(alike, got):
                found[k] = b
    numbers = iter(range(len(leaves)))
    return jax.tree.map(lambda _: found[next(numbers)], array)


def combined_all_2(array, axis, combine):
    pieces = gathered_by_type(array, axis)
    return folded_in_pairs(pieces, combine)


def joined_along(blocks, dim):
    lengths = list(blocks.shape[1:])
    lengths[dim] *= blocks.shape[0]
    return jnp.moveaxis(blocks, 0, dim).reshape(lengths)


def collect(array, axis, dim):
    return joined_along(sent_to_all(array, axis), dim)


def split_up(array, dim, size):
    lengths = array.shape
    blocks = array.reshape(*lengths[:dim], size, lengths[dim] // size, *lengths[dim + 1 :])
    return jnp.moveaxis(blocks, dim, 0)


def summed_on_arrival(array, axis, dim):
    blocks = split_up(array, dim, lax.axis_size(axis))
    arrived = lax.all_to_all(blocks, axis, split_axis=0, concat_axis=0, tiled=True)
    return arrived.sum(axis=0)


def combine(first, second):
    higher = jnp.maximum(first[0], second[0])
    return (higher, first[1] * jnp.exp(first[0] - higher) + second[1] * jnp.exp(second[0] - higher))


def reduce_rows(top, total):
    higher, whole = combined_all((top, total), "tgt", combine)
    return -(higher + jnp.log(whole))


def reduce_cols(top, total):
    higher, whole = combined_all_2((top, total), "src", combine)
    return -(higher + jnp.log(whole))


def body(source_words, target_words):
    width = source_words.shape[1]
    scale = 4.0 / math.sqrt(width)
    highest = lax.Precision.HIGHEST
    src_block = collect(source_words, "tgt", 0)
    rows = src_block.shape[0]
    cols = target_words.shape[0] * lax.axis_size("src")
    inner = (((1,), (1,)), ((), ()))
    leading = (((0,), (0,)), ((), ()))

    def scores(piece):
        return lax.dot_general(src_block, piece, inner, preferred_element_type=jnp.float32) * scale

    col_pot = jnp.zeros((cols,), jnp.float32)
    row_pot = jnp.zeros((rows,), jnp.float32)
    for sweep_index in range(ITERS):
        row_top = jnp.full((rows,), -jnp.inf, jnp.float32)
        total = jnp.zeros((rows,), jnp.float32)
        row_shift = col_pot
        row_logits = scores(collect(target_words, "src", 0)) + row_shift[None, :]
        higher = jnp.maximum(row_top, jnp.max(row_logits, axis=1))
        total = total * jnp.exp(row_top - higher) + jnp.sum(
            jnp.exp(row_logits - higher[:, None]), axis=1
        )
        top, total = (higher, total)
        row_pot = reduce_rows(top, total)
        logits = scores(collect(target_words, "src", 0)) + row_pot[:, None]
        col_top = jnp.max(logits, axis=0)
        parts = jnp.stack([col_top, jnp.sum(jnp.exp(logits - col_top[None, :]), axis=0)])
        col_pot = reduce_cols(parts[0], parts[1])
    piece = collect(target_words, "src", 0)
    plan = jnp.exp(scores(piece) + row_pot[:, None] + col_pot[None, :]).astype(jnp.bfloat16)
    summed = jnp.dot(plan, piece, preferred_element_type=jnp.float32)
    matched = summed_on_arrival(summed, "tgt", 0)
    term = lax.dot_general(src_block.astype(jnp.float32), summed, leading, precision=highest)
    cov = lax.psum(term, ("src", "tgt"))
    ortho = cov / jnp.sqrt(jnp.sum(cov * cov) + 1e-06)
    for step_index in range(NEWTON):
        ortho = 1.5 * ortho - 0.5 * jnp.dot(
            ortho, jnp.dot(ortho.T, ortho, precision=highest), precision=highest
        )
    rotated = jnp.dot(source_words.astype(jnp.float32), ortho, precision=highest).astype(
        jnp.bfloat16
    )
    own_rows = rows // lax.axis_size("tgt")
    own_cols = cols // lax.axis_size("src")
    row_part = lax.dynamic_slice_in_dim(row_pot, lax.axis_index("tgt") * own_rows, own_rows)
    col_part = lax.dynamic_slice_in_dim(col_pot, lax.axis_index("src") * own_cols, own_cols)
    return (rotated, matched, ortho, row_part, col_part)


def solution(mesh):
    in_specs = (P(("src", "tgt"), None), P(("tgt", "src"), None))
    out_specs = (
        P(("src", "tgt"), None),
        P(("src", "tgt"), None),
        P(),
        P(("src", "tgt")),
        P(("tgt", "src")),
    )
    return jax.shard_map(body, mesh=mesh, in_specs=in_specs, out_specs=out_specs, check_vma=False)
```

profile of v0, /device:TPU:2, one launch (start us, length us, event | category | flops | bytes accessed | tf_op | source)
XLA Modules:
  0.0 516.1 jit_solution(17925122348003594462)
XLA Ops:
  7.2 1.0 broadcast_in_dim.12
  8.2 23.0 %all_to_all.39 = bf16[16,128,300]{1,2,0:T(8,128)(2,1)S(1)} all-to-all(bf16[16,128,300]{1,2,0:T(8,128)(2,1)S(1)} %broadcast_in_dim.12), channel_id=1, replica_groups=mesh['src'=16,'tgt'=16] {'tgt'}, dimensions={0} | all-to-all | bytes 2457600 | tf_op jit(solution)/shard_map/all_to_all | solution.py:13
  31.2 2.1 broadcast_in_dim.13
  33.3 10.1 %all-to-all-start.1 = ((bf16[16,120,300]{1,2,0:T(8,128)(2,1)}), bf16[16,120,300]{1,2,0:T(8,128)(2,1)S(1)}, u32[]{:S(2)}, u32[]{:S(2)}) async-start(bf16[16,120,300]{1,2,0:T(8,128)(2,1)} %broadcast_in_dim.13), calls=%async_computation.1 | async-start | bytes 2490368 | tf_op jit(solution)/shard_map/all_to_all | solution.py:13
  43.4 0.3 copy.93
  43.8 0.2 pad.8
  44.0 0.3 copy.82
  44.3 32.0 %all-to-all-done.1 = bf16[16,120,300]{1,2,0:T(8,128)(2,1)S(1)} async-done(((bf16[16,120,300]{1,2,0:T(8,128)(2,1)}), bf16[16,120,300]{1,2,0:T(8,128)(2,1)S(1)}, u32[]{:S(2)}, u32[]{:S(2)}) %all-to-all-start.1) | async-done | bytes 1152032 | tf_op jit(solution)/shard_map/all_to_all | solution.py:13
  76.4 1.4 copy.43
  77.7 2.7 reshape.145
  80.5 8.0 %fusion.30 = (f32[2048]{0:T(1024)S(1)}, f32[2048,1920]{1,0:T(8,128)}) fusion(bf16[2048,300]{0,1:T(8,128)(2,1)S(1)} %bitcast.103, bf16[1920,300]{0,1:T(8,128)(2,1)S(1)} %reshape.145), kind=kOutput, calls=%fused_computation.101 | convolution fusion | flops 2367158272 | bytes 18117632 | tf_op jit(solution)/shard_map/dot_general | solution.py:115
  88.4 7.7 %exponential_reduce_fusion.3 = f32[2048]{0:T(1024)S(1)} fusion(f32[2048,1920]{1,0:T(8,128)} %get-tuple-element.55, f32[2048]{0:T(1024)S(1)} %get-tuple-element.54), kind=kLoop, calls=%fused_computation.4 | loop fusion | flops 7862272 | bytes 15745024 | tf_op jit(solution)/shard_map/reduce_sum | solution.py:125
  96.2 11.4 %all_to_all.40 = f32[16,2,2048]{2,1,0:T(2,128)S(1)} all-to-all(f32[16,2,2048]{2,1,0:T(2,128)S(1)} %broadcast_in_dim.14), channel_id=1, replica_groups=mesh['src'=16,'tgt'=16] {'tgt'}, dimensions={0} | all-to-all | bytes 524288 | tf_op jit(solution)/shard_map/all_to_all | solution.py:13
  107.6 0.2 fusion.27
  108.5 6.6 %add_reduce_fusion.1 = f32[1920]{0:T(1024)S(1)} fusion(f32[2048,1920]{1,0:T(8,128)} %get-tuple-element.55, f32[2048]{0:T(1024)S(1)} %bitcast.127), kind=kLoop, calls=%fused_computation.6 | loop fusion | flops 7862400 | bytes 15744512 | tf_op jit(solution)/shard_map/reduce_max | solution.py:131
  115.0 8.1 %exponential_reduce_fusion.2 = f32[1920]{0:T(1024)S(1)} fusion(f32[2048,1920]{1,0:T(8,128)} %get-tuple-element.55, f32[1920]{0:T(1024)S(1)} %add_reduce_fusion.1, f32[2048]{0:T(1024)S(1)} %bitcast.128), kind=kLoop, calls=%fused_computation.3 | loop fusion | flops 11794560 | bytes 15752192 | tf_op jit(solution)/shard_map/reduce_sum | solution.py:132
  123.3 15.1 %all_to_all.41 = f32[16,2,1920]{2,1,0:T(2,128)S(1)} all-to-all(f32[16,2,1920]{2,1,0:T(2,128)S(1)} %broadcast_in_dim.15), channel_id=1, replica_groups=mesh['src'=16,'tgt'=16] {'src'}, dimensions={0} | all-to-all | bytes 491520 | tf_op jit(solution)/shard_map/all_to_all | solution.py:13
  138.4 0.2 fusion.29
  139.2 6.6 %add_reduce_fusion = f32[2048]{0:T(1024)S(1)} fusion(f32[2048,1920]{1,0:T(8,128)} %get-tuple-element.55, f32[1920]{0:T(1024)S(1)} %negate_reduce_fusion), kind=kLoop, calls=%fused_computation.5 | loop fusion | flops 7862272 | bytes 15744512 | tf_op jit(solution)/shard_map/reduce_max | solution.py:124
  145.7 8.2 %exponential_reduce_fusion.1 = f32[2048]{0:T(1024)S(1)} fusion(f32[2048,1920]{1,0:T(8,128)} %get-tuple-element.55, f32[2048]{0:T(1024)S(1)} %add_reduce_fusion, f32[1920]{0:T(1024)S(1)} %negate_reduce_fusion), kind=kLoop, calls=%fused_computation.2 | loop fusion | flops 11794432 | bytes 15752704 | tf_op jit(solution)/shard_map/reduce_sum | solution.py:125
  154.1 11.6 %all_to_all.42 = f32[16,2,2048]{2,1,0:T(2,128)S(1)} all-to-all(f32[16,2,2048]{2,1,0:T(2,128)S(1)} %broadcast_in_dim.16), channel_id=1, replica_groups=mesh['src'=16,'tgt'=16] {'tgt'}, dimensions={0} | all-to-all | bytes 524288 | tf_op jit(solution)/shard_map/all_to_all | solution.py:13
  165.7 0.2 fusion.26
  166.5 6.6 %add_reduce_fusion.2 = f32[1920]{0:T(1024)S(1)} fusion(f32[2048,1920]{1,0:T(8,128)} %get-tuple-element.55, f32[2048]{0:T(1024)S(1)} %bitcast.124), kind=kLoop, calls=%fused_computation.7 | loop fusion | flops 7862400 | bytes 15744512 | tf_op jit(solution)/shard_map/reduce_max | solution.py:131
  173.1 8.1 %exponential_reduce_fusion = f32[1920]{0:T(1024)S(1)} fusion(f32[2048,1920]{1,0:T(8,128)} %get-tuple-element.55, f32[1920]{0:T(1024)S(1)} %add_reduce_fusion.2, f32[2048]{0:T(1024)S(1)} %bitcast.125), kind=kLoop, calls=%fused_computation.1 | loop fusion | flops 11794560 | bytes 15752192 | tf_op jit(solution)/shard_map/reduce_sum | solution.py:132
  181.3 0.8 broadcast_in_dim.17
  182.1 4.3 all-to-all-start.5
  186.4 0.5 dynamic-slice_bitcast_fusion.1
  186.9 10.8 %all-to-all-done.5 = f32[16,2,1920]{2,1,0:T(2,128)S(1)} async-done(((f32[16,2,1920]{2,1,0:T(2,128)}), f32[16,2,1920]{2,1,0:T(2,128)S(1)}, u32[]{:S(2)}, u32[]{:S(2)}) %all-to-all-start.5) | async-done | bytes 245792 | tf_op jit(solution)/shard_map/all_to_all | solution.py:13
  197.7 0.2 fusion.28
  198.5 9.8 %fusion = f32[2048,300]{0,1:T(8,128)} fusion(bf16[1920,300]{0,1:T(8,128)(2,1)S(1)} %reshape.145, f32[2048,1920]{1,0:T(8,128)} %get-tuple-element.55, f32[1920]{0:T(1024)S(1)} %get-tuple-element.20, f32[2048]{0:T(1024)S(1)} %bitcast.126), kind=kOutput, calls=%fused_computation.9 | convolution fusion | flops 2371092480 | bytes 19354112 | tf_op jit(solution)/shard_map/dot_general | solution.py:136
  208.3 4.6 convolution_bitcast_fusion
  212.8 2.2 copy.83
  215.2 2.2 copy.60
  217.4 4.9 all-to-all-start.6
  222.3 0.6 dynamic-slice_bitcast_fusion
  222.9 250.2 %all-reduce.2.cloned.1.call-done = f32[300,300]{0,1:T(8,128)} async-done(((f32[300,300]{0,1:T(8,128)}), f32[300,300]{0,1:T(8,128)}) %all-reduce.2.cloned.1.call-update) | async-done | bytes 360016 | tf_op jit(solution)/shard_map/psum | solution.py:139
  473.1 1.7 multiply_reduce_fusion
  475.6 2.2 fusion.16
  477.8 2.4 fusion.14
  480.3 1.0 fusion.31
  481.3 1.2 fusion.13
  482.6 1.0 fusion.32
  483.6 1.3 fusion.12
  484.9 1.0 fusion.33
  485.9 1.2 fusion.11
  487.1 1.0 fusion.34
  488.2 1.3 fusion.10
  489.5 1.3 fusion.35
  490.7 1.2 fusion.9
  492.0 1.0 fusion.36
  493.0 1.3 fusion.8
  494.3 1.0 fusion.37
  495.3 1.2 fusion.7
  496.6 1.0 fusion.38
  497.6 1.3 fusion.6
  498.9 1.0 fusion.39
  499.9 1.2 fusion.5
  501.2 1.0 fusion.40
  502.2 1.5 fusion.4
  503.8 1.0 fusion.41
  504.8 1.2 fusion.3
  506.0 1.0 copy.61
  507.0 1.0 fusion.15
  508.0 0.8 reduce_sum.65
  (90 shorter events, 2.8 us)
Async XLA Ops:
  33.3 43.0 %all-to-all-start.1 = ((bf16[16,120,300]{1,2,0:T(8,128)(2,1)}), bf16[16,120,300]{1,2,0:T(8,128)(2,1)S(1)}, u32[]{:S(2)}, u32[]{:S(2)}) async-start(bf16[16,120,300]{1,2,0:T(8,128)(2,1)} %broadcast_in_dim.13), calls=%async_computation.1 | async-start | bytes 2490368 | tf_op jit(solution)/shard_map/all_to_all | solution.py:13
  182.1 15.6 %all-to-all-start.5 = ((f32[16,2,1920]{2,1,0:T(2,128)}), f32[16,2,1920]{2,1,0:T(2,128)S(1)}, u32[]{:S(2)}, u32[]{:S(2)}) async-start(f32[16,2,1920]{2,1,0:T(2,128)} %broadcast_in_dim.17), calls=%async_computation.5 | async-start | bytes 491520 | tf_op jit(solution)/shard_map/all_to_all | solution.py:13
  186.4 286.8 %all-reduce.2.cloned.1.call-start = ((), (), s32[]{:S(2)}) async-start(), calls=%async_computation.7 | async-start | bytes 933888 | tf_op jit(solution)/shard_map/psum | solution.py:139
  217.4 290.6 %all-to-all-start.6 = ((f32[16,128,300]{1,2,0:T(8,128)}), f32[16,128,300]{1,2,0:T(8,128)S(1)}, u32[]{:S(2)}, u32[]{:S(2)}) async-start(f32[16,128,300]{1,2,0:T(8,128)} %copy.60), calls=%async_computation.6 | async-start | bytes 4980736 | tf_op jit(solution)/shard_map/all_to_all | solution.py:85
  480.2 26.8 %copy-start = (bf16[128,300]{0,1:T(8,128)(2,1)S(1)}, bf16[128,300]{0,1:T(8,128)(2,1)}, u32[]{:S(2)}) copy-start(bf16[128,300]{0,1:T(8,128)(2,1)} %param.2) | copy-start | bytes 230404
Sparse Core Ops, SparseCore 0:
  213.0 260.1 all-reduce.1
where the time goes:
time: 523 us; the launch traced here: 516 us
  waiting for transfers between devices  293 us (56%)
  blocking collectives  61.2 us (12%)
  other arithmetic  55 us (11%)
  matrix products  53.5 us (10%)
  starting transfers between devices  19.4 us (4%)
  local copies, waits for them, and re-layouts  18.1 us (3%)
  between operations  15.8 us (3%)
    psum x1, waiting for transfers between devices, body(): cov = lax.psum(term, ('src', 'tgt'))  250 us
    all_to_all x4, blocking collectives, sent_to_all(): return lax.all_to_all(copies, axis, split_axis=0, concat_axis=0, tiled=True)  61.2 us
    all_to_all x2, waiting for transfers between devices, sent_to_all(): return lax.all_to_all(copies, axis, split_axis=0, concat_axis=0, tiled=True)  42.8 us
    dot_general x12, matrix products, body(): jnp.dot(ortho, jnp.dot(ortho.T, ortho, precision=highest), precision=high...  16.4 us
    reduce_sum x2, other arithmetic, body(): jnp.sum(jnp.exp(logits - col_top[None, :]), axis=0)  16.2 us
    reduce_sum x2, other arithmetic, body(): jnp.sum(jnp.exp(row_logits - higher[:, None]), axis=1)  15.8 us
    all_to_all x2, starting transfers between devices, sent_to_all(): return lax.all_to_all(copies, axis, split_axis=0, concat_axis=0, tiled=True)  14.4 us
    dot_general x12, matrix products, body(): jnp.dot(ortho.T, ortho, precision=highest)  13.8 us
  transfers between devices with their start and end apart: 4, of which 3 were waited for; matrix products, arithmetic and copies ran while one was open for 8% of the time, Pallas kernels for 0%

commit v1 on v0

--- a/solution.py
+++ b/solution.py
@@ -136,7 +136,7 @@
     summed = jnp.dot(plan, piece, preferred_element_type=jnp.float32)
     matched = summed_on_arrival(summed, "tgt", 0)
     term = lax.dot_general(src_block.astype(jnp.float32), summed, leading, precision=highest)
-    cov = lax.psum(term, ("src", "tgt"))
+    cov = lax.psum(lax.psum(term, "tgt"), "src")
     ortho = cov / jnp.sqrt(jnp.sum(cov * cov) + 1e-06)
     for step_index in range(NEWTON):
         ortho = 1.5 * ortho - 0.5 * jnp.dot(

time: 523 us -> 541 us (1.034)
  blocking collectives: 61.2 us -> 76.6 us
  waiting for transfers between devices: 293 us -> 299 us
    psum x1 -> x2, waiting for transfers between devices: 250 us -> 267 us  [body(): cov = lax.psum(lax.psum(term, 'tgt'), 'src')]
    all_to_all x4 -> x5, blocking collectives: 61.2 us -> 76.6 us  [sent_to_all(): return lax.all_to_all(copies, axis, split_axis=0, concat_axis=0, tiled=True)]
    all_to_all x2 -> x1, waiting for transfers between devices: 42.8 us -> 32 us  [sent_to_all(): return lax.all_to_all(copies, axis, split_axis=0, concat_axis=0, tiled=True)]
    all_to_all x2 -> x1, starting transfers between devices: 14.4 us -> 10.1 us  [sent_to_all(): return lax.all_to_all(copies, axis, split_axis=0, concat_axis=0, tiled=True)]
where the time goes in v1:
time: 541 us; the launch traced here: 533 us
  waiting for transfers between devices  299 us (55%)
  blocking collectives  76.6 us (14%)
  other arithmetic  55 us (10%)
  matrix products  53.5 us (10%)
  local copies, waits for them, and re-layouts  17.4 us (3%)
  between operations  15.8 us (3%)
  starting transfers between devices  15.2 us (3%)
    psum x2, waiting for transfers between devices, body(): cov = lax.psum(lax.psum(term, 'tgt'), 'src')  267 us
    all_to_all x5, blocking collectives, sent_to_all(): return lax.all_to_all(copies, axis, split_axis=0, concat_axis=0, tiled=True)  76.6 us
    all_to_all x1, waiting for transfers between devices, sent_to_all(): return lax.all_to_all(copies, axis, split_axis=0, concat_axis=0, tiled=True)  32 us
    dot_general x12, matrix products, body(): jnp.dot(ortho, jnp.dot(ortho.T, ortho, precision=highest), precision=high...  16.4 us
    reduce_sum x2, other arithmetic, body(): jnp.sum(jnp.exp(logits - col_top[None, :]), axis=0)  16.2 us
    reduce_sum x2, other arithmetic, body(): jnp.sum(jnp.exp(row_logits - higher[:, None]), axis=1)  15.8 us
    dot_general x12, matrix products, body(): jnp.dot(ortho.T, ortho, precision=highest)  13.8 us
    reduce_max x2, other arithmetic, body(): col_top = jnp.max(logits, axis=0)  13.1 us
  transfers between devices with their start and end apart: 4, of which 3 were waited for; matrix products, arithmetic and copies ran while one was open for 8% of the time, Pallas kernels for 0%

profile of v1, /device:TPU:2, one launch (start us, length us, event | category | flops | bytes accessed | tf_op | source)
XLA Modules:
  0.0 533.0 jit_solution(13960925923211708584)
XLA Ops:
  7.2 1.0 broadcast_in_dim.12
  8.2 23.0 %all_to_all.39 = bf16[16,128,300]{1,2,0:T(8,128)(2,1)S(1)} all-to-all(bf16[16,128,300]{1,2,0:T(8,128)(2,1)S(1)} %broadcast_in_dim.12), channel_id=1, replica_groups=mesh['src'=16,'tgt'=16] {'tgt'}, dimensions={0} | all-to-all | bytes 2457600 | tf_op jit(solution)/shard_map/all_to_all | solution.py:13
  31.2 2.1 broadcast_in_dim.13
  33.3 10.1 %all-to-all-start.1 = ((bf16[16,120,300]{1,2,0:T(8,128)(2,1)}), bf16[16,120,300]{1,2,0:T(8,128)(2,1)S(1)}, u32[]{:S(2)}, u32[]{:S(2)}) async-start(bf16[16,120,300]{1,2,0:T(8,128)(2,1)} %broadcast_in_dim.13), calls=%async_computation.1 | async-start | bytes 2490368 | tf_op jit(solution)/shard_map/all_to_all | solution.py:13
  43.5 0.3 copy.93
  43.8 0.2 pad.8
  44.0 0.3 copy.82
  44.4 32.0 %all-to-all-done.1 = bf16[16,120,300]{1,2,0:T(8,128)(2,1)S(1)} async-done(((bf16[16,120,300]{1,2,0:T(8,128)(2,1)}), bf16[16,120,300]{1,2,0:T(8,128)(2,1)S(1)}, u32[]{:S(2)}, u32[]{:S(2)}) %all-to-all-start.1) | async-done | bytes 1152032 | tf_op jit(solution)/shard_map/all_to_all | solution.py:13
  76.4 1.4 copy.43
  77.7 2.7 reshape.145
  80.5 8.0 %fusion.30 = (f32[2048]{0:T(1024)S(1)}, f32[2048,1920]{1,0:T(8,128)}) fusion(bf16[2048,300]{0,1:T(8,128)(2,1)S(1)} %bitcast.103, bf16[1920,300]{0,1:T(8,128)(2,1)S(1)} %reshape.145), kind=kOutput, calls=%fused_computation.101 | convolution fusion | flops 2367158272 | bytes 18117632 | tf_op jit(solution)/shard_map/dot_general | solution.py:115
  88.4 7.7 %exponential_reduce_fusion.3 = f32[2048]{0:T(1024)S(1)} fusion(f32[2048,1920]{1,0:T(8,128)} %get-tuple-element.55, f32[2048]{0:T(1024)S(1)} %get-tuple-element.54), kind=kLoop, calls=%fused_computation.4 | loop fusion | flops 7862272 | bytes 15745024 | tf_op jit(solution)/shard_map/reduce_sum | solution.py:125
  96.2 11.4 %all_to_all.40 = f32[16,2,2048]{2,1,0:T(2,128)S(1)} all-to-all(f32[16,2,2048]{2,1,0:T(2,128)S(1)} %broadcast_in_dim.14), channel_id=1, replica_groups=mesh['src'=16,'tgt'=16] {'tgt'}, dimensions={0} | all-to-all | bytes 524288 | tf_op jit(solution)/shard_map/all_to_all | solution.py:13
  107.6 0.2 fusion.27
  108.5 6.6 %add_reduce_fusion.1 = f32[1920]{0:T(1024)S(1)} fusion(f32[2048,1920]{1,0:T(8,128)} %get-tuple-element.55, f32[2048]{0:T(1024)S(1)} %bitcast.127), kind=kLoop, calls=%fused_computation.6 | loop fusion | flops 7862400 | bytes 15744512 | tf_op jit(solution)/shard_map/reduce_max | solution.py:131
  115.0 8.1 %exponential_reduce_fusion.2 = f32[1920]{0:T(1024)S(1)} fusion(f32[2048,1920]{1,0:T(8,128)} %get-tuple-element.55, f32[1920]{0:T(1024)S(1)} %add_reduce_fusion.1, f32[2048]{0:T(1024)S(1)} %bitcast.128), kind=kLoop, calls=%fused_computation.3 | loop fusion | flops 11794560 | bytes 15752192 | tf_op jit(solution)/shard_map/reduce_sum | solution.py:132
  123.3 15.1 %all_to_all.41 = f32[16,2,1920]{2,1,0:T(2,128)S(1)} all-to-all(f32[16,2,1920]{2,1,0:T(2,128)S(1)} %broadcast_in_dim.15), channel_id=1, replica_groups=mesh['src'=16,'tgt'=16] {'src'}, dimensions={0} | all-to-all | bytes 491520 | tf_op jit(solution)/shard_map/all_to_all | solution.py:13
  138.4 0.2 fusion.29
  139.2 6.6 %add_reduce_fusion = f32[2048]{0:T(1024)S(1)} fusion(f32[2048,1920]{1,0:T(8,128)} %get-tuple-element.55, f32[1920]{0:T(1024)S(1)} %negate_reduce_fusion), kind=kLoop, calls=%fused_computation.5 | loop fusion | flops 7862272 | bytes 15744512 | tf_op jit(solution)/shard_map/reduce_max | solution.py:124
  145.7 8.2 %exponential_reduce_fusion.1 = f32[2048]{0:T(1024)S(1)} fusion(f32[2048,1920]{1,0:T(8,128)} %get-tuple-element.55, f32[2048]{0:T(1024)S(1)} %add_reduce_fusion, f32[1920]{0:T(1024)S(1)} %negate_reduce_fusion), kind=kLoop, calls=%fused_computation.2 | loop fusion | flops 11794432 | bytes 15752704 | tf_op jit(solution)/shard_map/reduce_sum | solution.py:125
  154.1 11.6 %all_to_all.42 = f32[16,2,2048]{2,1,0:T(2,128)S(1)} all-to-all(f32[16,2,2048]{2,1,0:T(2,128)S(1)} %broadcast_in_dim.16), channel_id=1, replica_groups=mesh['src'=16,'tgt'=16] {'tgt'}, dimensions={0} | all-to-all | bytes 524288 | tf_op jit(solution)/shard_map/all_to_all | solution.py:13
  165.7 0.2 fusion.26
  166.5 6.6 %add_reduce_fusion.2 = f32[1920]{0:T(1024)S(1)} fusion(f32[2048,1920]{1,0:T(8,128)} %get-tuple-element.55, f32[2048]{0:T(1024)S(1)} %bitcast.124), kind=kLoop, calls=%fused_computation.7 | loop fusion | flops 7862400 | bytes 15744512 | tf_op jit(solution)/shard_map/reduce_max | solution.py:131
  173.1 8.1 %exponential_reduce_fusion = f32[1920]{0:T(1024)S(1)} fusion(f32[2048,1920]{1,0:T(8,128)} %get-tuple-element.55, f32[1920]{0:T(1024)S(1)} %add_reduce_fusion.2, f32[2048]{0:T(1024)S(1)} %bitcast.125), kind=kLoop, calls=%fused_computation.1 | loop fusion | flops 11794560 | bytes 15752192 | tf_op jit(solution)/shard_map/reduce_sum | solution.py:132
  181.4 15.4 %all_to_all.43 = f32[16,2,1920]{2,1,0:T(2,128)S(1)} all-to-all(f32[16,2,1920]{2,1,0:T(2,128)S(1)} %broadcast_in_dim.17), channel_id=1, replica_groups=mesh['src'=16,'tgt'=16] {'src'}, dimensions={0} | all-to-all | bytes 491520 | tf_op jit(solution)/shard_map/all_to_all | solution.py:13
  196.8 0.2 fusion.28
  197.6 9.8 %fusion = f32[2048,300]{0,1:T(8,128)} fusion(bf16[1920,300]{0,1:T(8,128)(2,1)S(1)} %reshape.145, f32[2048,1920]{1,0:T(8,128)} %get-tuple-element.55, f32[1920]{0:T(1024)S(1)} %get-tuple-element.20, f32[2048]{0:T(1024)S(1)} %bitcast.126), kind=kOutput, calls=%fused_computation.9 | convolution fusion | flops 2371092480 | bytes 19354112 | tf_op jit(solution)/shard_map/dot_general | solution.py:136
  207.4 4.6 convolution_bitcast_fusion
  212.0 0.5 dynamic-slice_bitcast_fusion.1
  212.5 2.2 copy.83
  214.7 115.1 %all-reduce.3.cloned.1.call-done = f32[300,300]{0,1:T(8,128)} async-done(((f32[300,300]{0,1:T(8,128)}), f32[300,300]{0,1:T(8,128)}) %all-reduce.3.cloned.1.call-update) | async-done | bytes 360016 | tf_op jit(solution)/shard_map/psum | solution.py:139
  329.8 0.2 slice_bitcast_fusion
  330.0 2.2 copy.60
  332.2 5.0 all-to-all-start.6
  337.2 0.6 dynamic-slice_bitcast_fusion
  337.8 152.2 %all-reduce.5.cloned.1.call-done = f32[300,300]{0,1:T(8,128)} async-done(((f32[300,300]{0,1:T(8,128)}), f32[300,300]{0,1:T(8,128)}) %all-reduce.5.cloned.1.call-update) | async-done | bytes 360016 | tf_op jit(solution)/shard_map/psum | solution.py:139
  490.0 1.7 multiply_reduce_fusion
  492.5 2.2 fusion.16
  494.7 2.4 fusion.14
  497.1 1.0 fusion.31
  498.2 1.2 fusion.13
  499.4 1.0 fusion.32
  500.5 1.3 fusion.12
  501.7 1.0 fusion.33
  502.8 1.2 fusion.11
  504.0 1.0 fusion.34
  505.1 1.3 fusion.10
  506.4 1.3 fusion.35
  507.6 1.2 fusion.9
  508.9 1.0 fusion.36
  509.9 1.3 fusion.8
  511.2 1.0 fusion.37
  512.2 1.2 fusion.7
  513.5 1.0 fusion.38
  514.5 1.3 fusion.6
  515.8 1.0 fusion.39
  516.8 1.2 fusion.5
  518.1 1.0 fusion.40
  519.1 1.5 fusion.4
  520.7 1.0 fusion.41
  521.7 1.2 fusion.3
  522.9 1.0 copy.61
  523.9 1.0 fusion.15
  524.9 0.8 reduce_sum.65
  (92 shorter events, 2.8 us)
Async XLA Ops:
  33.3 43.0 %all-to-all-start.1 = ((bf16[16,120,300]{1,2,0:T(8,128)(2,1)}), bf16[16,120,300]{1,2,0:T(8,128)(2,1)S(1)}, u32[]{:S(2)}, u32[]{:S(2)}) async-start(bf16[16,120,300]{1,2,0:T(8,128)(2,1)} %broadcast_in_dim.13), calls=%async_computation.1 | async-start | bytes 2490368 | tf_op jit(solution)/shard_map/all_to_all | solution.py:13
  43.4 286.3 %all-reduce.3.cloned.1.call-start = ((), (), s32[]{:S(2)}) async-start(), calls=%async_computation.7 | async-start | bytes 933888 | tf_op jit(solution)/shard_map/psum | solution.py:139
  212.0 278.1 %all-reduce.5.cloned.1.call-start = ((), (), s32[]{:S(2)}) async-start(), calls=%async_computation.8 | async-start | bytes 933888 | tf_op jit(solution)/shard_map/psum | solution.py:139
  332.2 192.7 %all-to-all-start.6 = ((f32[16,128,300]{1,2,0:T(8,128)}), f32[16,128,300]{1,2,0:T(8,128)S(1)}, u32[]{:S(2)}, u32[]{:S(2)}) async-start(f32[16,128,300]{1,2,0:T(8,128)} %copy.60), calls=%async_computation.6 | async-start | bytes 4980736 | tf_op jit(solution)/shard_map/all_to_all | solution.py:85
  497.1 26.8 %copy-start = (bf16[128,300]{0,1:T(8,128)(2,1)S(1)}, bf16[128,300]{0,1:T(8,128)(2,1)}, u32[]{:S(2)}) copy-start(bf16[128,300]{0,1:T(8,128)(2,1)} %param.2) | copy-start | bytes 230404
Sparse Core Ops, SparseCore 0:
  212.1 117.6 all-reduce.2
  332.4 157.5 all-reduce.4
